TPU v7x, 16 devices: a whole 2x2x2 slice. The times are simulated.
16 devices in a mesh: replica: 4 (over z, y), model: 4 (over x, core).
Axes of the slice: x: 2, y: 2, z: 2, core: 2. Of those that a mesh axis runs over, the one named last changes fastest.
Arguments:
- tokens: bfloat16 [512, 2304], P('replica'), parts along dimension 0
- lengths: int32 [512], P('replica'), parts along dimension 0
- k_cache: bfloat16 [512, 4, 512, 256], P('replica'), parts along dimension 0
- v_cache: bfloat16 [512, 4, 512, 256], P('replica'), parts along dimension 0
- norm_gain: bfloat16 [2304], replicated
- w_query: bfloat16 [2304, 2048], P(None, 'model')
- w_key: bfloat16 [2304, 1024], replicated
- w_value: bfloat16 [2304, 1024], replicated
- w_out: bfloat16 [2048, 2304], P('model')
- w_gate: bfloat16 [2304, 9216], P(None, 'model')
- w_up: bfloat16 [2304, 9216], P(None, 'model')
- w_down: bfloat16 [9216, 2304], P('model')
Outputs:
- output 1: bfloat16 [512, 2304], P('replica'), parts along dimension 0
- output 2: bfloat16 [512, 4, 256], P(('replica', 'model')), parts along dimension 0
- output 3: bfloat16 [512, 4, 256], P(('replica', 'model')), parts along dimension 0
There are 4 independent parts. A program takes and returns all parts, laid end to end along the dimension named above; an argument that names none is the same for every part.
All inputs are finite; a program needn't handle non-finite values.
Results may differ from a plain program's by a relative error of at most 0.0047526.
Values are sent between devices in bfloat16 or wider.
A program may use at most 1.25 GiB of HBM per device.

v0:
```python
import functools
import math
import jax
import jax.numpy as jnp
from jax import lax
from jax.experimental import pallas as pl
from jax.experimental.pallas import tpu as pltpu
from jax.sharding import PartitionSpec as P

ROPE_BASE = 10000.0
NORM_EPS = 1e-6
MASK_VALUE = -1e30
F32 = jnp.float32
BF16 = jnp.bfloat16

FIRST = 32
GROUP = 8
CHUNK = 128
UNROLL = 8
SLOTS = 12
COLS = 256
PIECE = 384


def iota(shape, dim):
    return lax.broadcasted_iota(jnp.int32, shape, dim)


def nt_dot(a, b):
    return lax.dot_general(a, b, (((1,), (1,)), ((), ())), preferred_element_type=F32)


def nn_dot(a, b):
    return jnp.dot(a, b, preferred_element_type=F32)


def interleave(first, second):
    pieces = []
    for r in range(0, first.shape[0], GROUP):
        pieces += [first[r:r + GROUP], second[r:r + GROUP]]
    return jnp.concatenate(pieces, axis=0)


def local_kernel(dims, len_hbm, x_hbm, gain_hbm, k_hbm, v_hbm, wq_hbm, wk_hbm, wv_hbm, wg_hbm, wu_hbm,
                 u_ref, o_ref, kv_ref,
                 len_s, len_v, x_v, gain_v, wq_v, wk_v, wv_v, wg_v, wu_v, kfirst, vfirst, kbuf, vbuf, h_v,
                 tile_s, q_rows, len_rows, s_first, s_buf, snew_v, vnew_v, m_v, l_v, acc_v,
                 sems, wsems, fsems, ksems, vsems):
    batch, model_dim, head_dim, context = dims
    half = head_dim // 2
    rows = 2 * GROUP
    groups = batch // GROUP
    me = lax.axis_index('model')
    n_pieces = wg_v.shape[0]
    last_start = context - CHUNK

    def piece_copy(hbm, buf, n, which):
        return pltpu.make_async_copy(hbm.at[:, pl.ds(n * COLS, COLS)], buf.at[n], wsems.at[which, n])

    def first_copy(hbm, buf, which, n):
        seqs = pl.ds(n * (batch // 2), batch // 2)
        return pltpu.make_async_copy(hbm.at[seqs, me, pl.ds(0, FIRST), :], buf.at[seqs], fsems.at[which, n])

    head_col = pl.multiple_of(me * head_dim, 128)
    small = [
        pltpu.make_async_copy(len_hbm, len_s, sems.at[0]),
        pltpu.make_async_copy(x_hbm, x_v, sems.at[1]),
        pltpu.make_async_copy(gain_hbm, gain_v, sems.at[2]),
        pltpu.make_async_copy(len_hbm, len_v, sems.at[6]),
        pltpu.make_async_copy(wq_hbm, wq_v, sems.at[3]),
        pltpu.make_async_copy(wk_hbm.at[:, pl.ds(head_col, head_dim)], wk_v, sems.at[4]),
        pltpu.make_async_copy(wv_hbm.at[:, pl.ds(head_col, head_dim)], wv_v, sems.at[5]),
    ]
    for copy in small:
        copy.start()
    for n in range(2):
        first_copy(k_hbm, kfirst, 0, n).start()
    for n in range(2):
        first_copy(v_hbm, vfirst, 1, n).start()
    for n in range(n_pieces):
        piece_copy(wg_hbm, wg_v, n, 0).start(priority=1)
        piece_copy(wu_hbm, wu_v, n, 1).start(priority=1)

    small[0].wait()

    def fill(r, t):
        for i in range(GROUP):
            b = r * GROUP + i
            for c in range((context - FIRST + CHUNK - 1) // CHUNK):
                tile_s[t + c] = b * 8 + c
            t = t + lax.shift_right_logical(len_s[0, b] + (CHUNK - 1 - FIRST), CHUNK.bit_length() - 1)
        return t
    tiles = lax.fori_loop(0, groups, fill, 0)
    for j in range(UNROLL):
        tile_s[tiles + j] = 7
    bodies = (tiles + UNROLL - 1) // UNROLL

    def issue(hbm, buf, bsems, body):
        slot = lax.rem(body, SLOTS)
        for j in range(UNROLL):
            code = tile_s[body * UNROLL + j]
            start = jnp.minimum(FIRST + (code & 7) * CHUNK, last_start)
            pltpu.make_async_copy(hbm.at[lax.shift_right_logical(code, 3), me, pl.ds(pl.multiple_of(start, FIRST), CHUNK), :],
                                  buf.at[slot, j], bsems.at[slot]).start()

    def issue_both(body, _):
        issue(k_hbm, kbuf, ksems, body)
        issue(v_hbm, vbuf, vsems, body)
        return 0

    def wait_body(buf, bsems, body):
        slot = lax.rem(body, SLOTS)
        pltpu.make_async_copy(buf.at[slot], buf.at[slot], bsems.at[slot]).wait()

    lax.fori_loop(0, jnp.minimum(bodies, SLOTS), issue_both, 0)

    small[3].wait()
    ii, jj = iota((batch, batch), 0), iota((batch, batch), 1)
    len_col = jnp.sum(jnp.where(ii == jj, len_v[...].astype(F32), 0.0), axis=1, keepdims=True)
    len_wide = jnp.broadcast_to(len_col, (batch, 128))
    len_rows[...] = interleave(len_wide, len_wide)
    freq = jnp.exp(iota((1, half), 1).astype(F32) * (-2.0 * math.log(ROPE_BASE) / head_dim))
    angles = len_col * freq
    cos_part, sin_part = jnp.cos(angles), jnp.sin(angles)

    def rope(v):
        a, b = v[:, :half], v[:, half:]
        return jnp.concatenate([a * cos_part - b * sin_part, b * cos_part + a * sin_part], axis=1).astype(BF16)

    small[1].wait()
    small[2].wait()
    x = x_v[...].astype(F32)
    mean_sq = jnp.mean(x * x, axis=-1, keepdims=True)
    h_v[...] = (x * lax.rsqrt(mean_sq + NORM_EPS) * gain_v[...].astype(F32).reshape(1, model_dim)).astype(BF16)

    small[4].wait()
    small[5].wait()
    small[6].wait()
    h = h_v[...]
    q = nn_dot(h, wq_v[...])
    k_new = rope(nn_dot(h, wk_v[...]))
    v_new = nn_dot(h, wv_v[...]).astype(BF16)
    kv_ref[:, :head_dim] = k_new
    kv_ref[:, head_dim:] = v_new
    vnew_v[...] = v_new.astype(F32)
    scale = head_dim ** -0.5
    q_heads = [rope(q[:, n * head_dim:(n + 1) * head_dim]).astype(F32) for n in range(2)]
    q_rows[...] = interleave(*q_heads).astype(BF16)
    k_wide = k_new.astype(F32)
    s_new = [jnp.broadcast_to(jnp.sum(qh * k_wide, axis=1, keepdims=True) * scale, (batch, 128)) for qh in q_heads]
    snew_v[...] = interleave(*s_new)

    lane, sub = iota((rows, GROUP * FIRST), 1), iota((rows, GROUP * FIRST), 0)
    own_lane = lax.shift_right_logical(lane, FIRST.bit_length() - 1) == (sub & (GROUP - 1))
    token = (lane & (FIRST - 1)).astype(F32)
    for n in range(2):
        first_copy(k_hbm, kfirst, 0, n).wait()
    for g in range(groups):
        keys = kfirst[g * GROUP:(g + 1) * GROUP].reshape(GROUP * FIRST, head_dim)
        s = nt_dot(q_rows[g * rows:(g + 1) * rows, :], keys)
        reach = len_rows[g * rows:(g + 1) * rows, :]
        s = jnp.where(own_lane & (token < jnp.concatenate([reach, reach], axis=1)), s * scale, MASK_VALUE)
        s_first[g] = s
        m_v[g * rows:(g + 1) * rows, :] = jnp.maximum(snew_v[g * rows:(g + 1) * rows, :], jnp.maximum(s[:, :128], s[:, 128:]))

    lane, sub = iota((rows, CHUNK), 1), iota((rows, CHUNK), 0) & (GROUP - 1)

    def tile_of(t):
        code = tile_s[t]
        b = lax.shift_right_logical(code, 3)
        row = pl.multiple_of(lax.shift_right_logical(b, GROUP.bit_length() - 1) * rows, rows)
        return b & (GROUP - 1), row, FIRST + (code & 7) * CHUNK

    def score_body(body, _):
        wait_body(kbuf, ksems, body)
        slot = lax.rem(body, SLOTS)
        scores = []
        for j in range(UNROLL):
            i, row, begin = tile_of(body * UNROLL + j)
            s = nt_dot(q_rows[pl.ds(row, rows), :], kbuf[slot, j])
            position = lane + jnp.minimum(begin, last_start)
            valid = (sub == i) & (position >= begin) & (position.astype(F32) < len_rows[pl.ds(row, rows), :])
            scores.append((row, jnp.where(valid, s * scale, MASK_VALUE)))
        for j, (row, s) in enumerate(scores):
            s_buf[body * UNROLL + j] = s
            m_v[pl.ds(row, rows), :] = jnp.maximum(m_v[pl.ds(row, rows), :], s)

        @pl.when(body + SLOTS < bodies)
        def _():
            issue(k_hbm, kbuf, ksems, body + SLOTS)
        return 0
    lax.fori_loop(0, bodies, score_body, 0)

    peak = jnp.max(m_v[...], axis=1, keepdims=True)
    m_v[...] = jnp.broadcast_to(peak, m_v.shape)

    for n in range(2):
        first_copy(v_hbm, vfirst, 1, n).wait()
    for g in range(groups):
        m = m_v[g * rows:(g + 1) * rows, :]
        p = jnp.exp(s_first[g] - jnp.concatenate([m, m], axis=1))
        l_v[g * rows:(g + 1) * rows, :] = p[:, :128] + p[:, 128:]
        acc_v[g * rows:(g + 1) * rows, :] = nn_dot(p.astype(BF16), vfirst[g * GROUP:(g + 1) * GROUP].reshape(GROUP * FIRST, head_dim))

    def value_body(body, _):
        wait_body(vbuf, vsems, body)
        slot = lax.rem(body, SLOTS)
        mixed = []
        for j in range(UNROLL):
            _, row, _ = tile_of(body * UNROLL + j)
            p = jnp.exp(s_buf[body * UNROLL + j] - m_v[pl.ds(row, rows), :])
            mixed.append((row, p, nn_dot(p.astype(BF16), vbuf[slot, j])))
        for row, p, o in mixed:
            l_v[pl.ds(row, rows), :] += p
            acc_v[pl.ds(row, rows), :] += o

        @pl.when(body + SLOTS < bodies)
        def _():
            issue(v_hbm, vbuf, vsems, body + SLOTS)
        return 0
    lax.fori_loop(0, bodies, value_body, 0)

    e_new = jnp.exp(snew_v[...] - m_v[...])
    total = jnp.sum(l_v[...], axis=1, keepdims=True) + e_new[:, :1]
    weight_new = e_new[:, :1].astype(BF16).astype(F32)
    mixed = (acc_v[...] + weight_new * interleave(vnew_v[...], vnew_v[...])) / total
    for head in range(2):
        o_head = jnp.concatenate([mixed[g * rows + head * GROUP:g * rows + (head + 1) * GROUP] for g in range(groups)], axis=0)
        o_ref[:, head * head_dim:(head + 1) * head_dim] = o_head.astype(BF16)

    for n in range(n_pieces):
        piece_copy(wg_hbm, wg_v, n, 0).wait()
        piece_copy(wu_hbm, wu_v, n, 1).wait()
        gate = nn_dot(h_v[...], wg_v[n])
        up = nn_dot(h_v[...], wu_v[n])
        u_ref[:, n * COLS:(n + 1) * COLS] = (gate * jax.nn.sigmoid(gate) * up).astype(BF16)


def reduce_kernel(dims, x_hbm, u_v, o_v, kv_v, wo_hbm, wd_hbm,
                  y_v, kn_ref, vn_ref,
                  x_v, kv_all, kv_rows, wo_v, wd_v, part, from_sib, half_sum, from_chip,
                  sems, wsems, kv_send, kv_recv, rs_send, rs_recv, xs_send, xs_recv, gx_send, gx_recv, gs_send, gs_recv, gf_send, gf_recv):
    batch, head_dim = dims
    quarter = batch // 4
    pieces = part.shape[0]
    me = lax.axis_index('model')
    chip, core = me // 2, me % 2
    sibling = chip * 2 + (1 - core)
    across = (1 - chip) * 2 + core

    def rows_of(chip_, core_):
        return pl.multiple_of(core_ * (2 * quarter) + chip_ * quarter, quarter)

    own = rows_of(chip, core)
    own_half = pl.multiple_of(core * (2 * quarter), 2 * quarter)
    sib_half = pl.multiple_of((1 - core) * (2 * quarter), 2 * quarter)

    def weight_copies(n):
        cols = pl.ds(n * PIECE, PIECE)
        return (pltpu.make_async_copy(wo_hbm.at[:, cols], wo_v.at[:, cols], wsems.at[0, n]),
                pltpu.make_async_copy(wd_hbm.at[:, cols], wd_v.at[:, cols], wsems.at[1, n]))

    x_copy = pltpu.make_async_copy(x_hbm.at[pl.ds(own, quarter), :], x_v, sems.at[0])
    for n in range(pieces):
        for copy in weight_copies(n):
            copy.start()
    x_copy.start()

    barrier = pltpu.get_barrier_semaphore()
    for d in range(1, 4):
        pl.semaphore_signal(barrier, inc=1, device_id={'model': (me + d) % 4}, device_id_type=pl.DeviceIdType.MESH)
    pl.semaphore_wait(barrier, 3)

    kv_sends = []
    for d in range(1, 4):
        to = (me + d) % 4
        kv_sends.append(pltpu.make_async_remote_copy(
            src_ref=kv_v.at[pl.ds(pl.multiple_of(to * quarter, quarter), quarter), :], dst_ref=kv_all.at[me],
            send_sem=kv_send.at[d - 1], recv_sem=kv_recv.at[d - 1], device_id={'model': to}, device_id_type=pl.DeviceIdType.MESH))
    for copy in kv_sends:
        copy.start()
    kv_all[me] = kv_v[pl.ds(pl.multiple_of(me * quarter, quarter), quarter), :]

    def remote(src, dst, send, recv, n, to):
        return pltpu.make_async_remote_copy(src_ref=src, dst_ref=dst, send_sem=send.at[n], recv_sem=recv.at[n],
                                            device_id={'model': to}, device_id_type=pl.DeviceIdType.MESH)

    def rs(n):
        return remote(part.at[n, pl.ds(sib_half, 2 * quarter), :], from_sib.at[n], rs_send, rs_recv, n, sibling)

    def xs(n):
        return remote(half_sum.at[n, pl.ds(pl.multiple_of((1 - chip) * quarter, quarter), quarter), :], from_chip.at[n], xs_send, xs_recv, n, across)

    def y_piece(row, n):
        return y_v.at[pl.ds(row, quarter), pl.ds(n * PIECE, PIECE)]

    def gx(n):
        return remote(y_piece(own, n), y_piece(own, n), gx_send, gx_recv, n, across)

    def gs(n):
        return remote(y_piece(own, n), y_piece(own, n), gs_send, gs_recv, n, sibling)

    def gf(n):
        other = rows_of(1 - chip, core)
        return remote(y_piece(other, n), y_piece(other, n), gf_send, gf_recv, n, sibling)

    def sum_chip(n):
        rs(n).wait_recv()
        half_sum[n] = part[n, pl.ds(own_half, 2 * quarter), :] + from_sib[n]
        xs(n).start()

    def finish(n):
        xs(n).wait_recv()
        cols = slice(n * PIECE, (n + 1) * PIECE)
        mine = half_sum[n, pl.ds(pl.multiple_of(chip * quarter, quarter), quarter), :] + from_chip[n]
        y_v[pl.ds(own, quarter), cols] = (x_v[:, cols].astype(F32) + mine).astype(BF16)
        gx(n).start()
        gs(n).start()

    def forward(n):
        gx(n).wait_recv()
        gf(n).start()

    for n in range(pieces):
        for copy in weight_copies(n):
            copy.wait()
        cols = slice(n * PIECE, (n + 1) * PIECE)
        part[n] = nn_dot(o_v[...], wo_v[:, cols]) + nn_dot(u_v[...], wd_v[:, cols])
        rs(n).start()
        if n >= 1:
            sum_chip(n - 1)
    sum_chip(pieces - 1)

    for copy in kv_sends:
        copy.wait_recv()
    for h in range(4):
        kv_rows[0, :, h, :] = kv_all[h, :, :head_dim].astype(F32)
        kv_rows[1, :, h, :] = kv_all[h, :, head_dim:].astype(F32)
    kn_ref[...] = kv_rows[0].astype(BF16)
    vn_ref[...] = kv_rows[1].astype(BF16)

    x_copy.wait()
    for n in range(pieces):
        finish(n)
    for n in range(pieces):
        forward(n)
    for n in range(pieces):
        gs(n).wait_recv()
        gf(n).wait_recv()

    for copy in kv_sends:
        copy.wait_send()
    for n in range(pieces):
        for copy in (rs(n), xs(n), gx(n), gs(n), gf(n)):
            copy.wait_send()


def solution(mesh):
    def local_step(tokens, lengths, k_cache, v_cache, norm_gain, w_query, w_key, w_value, w_out, w_gate, w_up, w_down):
        batch, model_dim = tokens.shape
        kv_heads, context, head_dim = k_cache.shape[1:]
        ffn = w_gate.shape[1]
        q_width = w_query.shape[1]
        rows = 2 * batch
        max_tiles = batch * (context // CHUNK) + UNROLL
        any_spec = pl.BlockSpec(memory_space=pl.ANY)
        vmem_spec = pl.BlockSpec(memory_space=pltpu.VMEM)
        dma = pltpu.SemaphoreType.DMA

        pieces = ffn // COLS
        hidden, attended, kv_new = pl.pallas_call(
            functools.partial(local_kernel, (batch, model_dim, head_dim, context)),
            name='attend_and_gate',
            out_shape=[pltpu.VMEM((batch, ffn), BF16), pltpu.VMEM((batch, q_width), BF16), pltpu.VMEM((batch, 2 * head_dim), BF16)],
            in_specs=[any_spec] * 10,
            out_specs=[vmem_spec] * 3,
            scratch_shapes=[
                pltpu.SMEM((1, batch), jnp.int32),
                pltpu.VMEM((1, batch), jnp.int32),
                pltpu.VMEM((batch, model_dim), BF16),
                pltpu.VMEM((model_dim,), BF16),
                pltpu.VMEM((model_dim, q_width), BF16),
                pltpu.VMEM((model_dim, head_dim), BF16),
                pltpu.VMEM((model_dim, head_dim), BF16),
                pltpu.VMEM((pieces, model_dim, COLS), BF16),
                pltpu.VMEM((pieces, model_dim, COLS), BF16),
                pltpu.VMEM((batch, FIRST, head_dim), BF16),
                pltpu.VMEM((batch, FIRST, head_dim), BF16),
                pltpu.VMEM((SLOTS, UNROLL, CHUNK, head_dim), BF16),
                pltpu.VMEM((SLOTS, UNROLL, CHUNK, head_dim), BF16),
                pltpu.VMEM((batch, model_dim), BF16),
                pltpu.SMEM((max_tiles,), jnp.int32),
                pltpu.VMEM((rows, head_dim), BF16),
                pltpu.VMEM((rows, 128), F32),
                pltpu.VMEM((batch // GROUP, 2 * GROUP, GROUP * FIRST), F32),
                pltpu.VMEM((max_tiles, 2 * GROUP, CHUNK), F32),
                pltpu.VMEM((rows, 128), F32),
                pltpu.VMEM((batch, head_dim), F32),
                pltpu.VMEM((rows, 128), F32),
                pltpu.VMEM((rows, 128), F32),
                pltpu.VMEM((rows, head_dim), F32),
                dma((7,)),
                dma((2, pieces)),
                dma((2, 2)),
                dma((SLOTS,)),
                dma((SLOTS,)),
            ],
            compiler_params=pltpu.CompilerParams(has_side_effects=True, vmem_limit_bytes=54 << 20),
        )(lengths.reshape(1, batch), tokens, norm_gain, k_cache, v_cache, w_query, w_key, w_value, w_gate, w_up)

        quarter = batch // 4
        pieces = model_dim // PIECE
        new_shape = (quarter, kv_heads, head_dim)
        out_shapes = [(batch, model_dim), new_shape, new_shape]
        return pl.pallas_call(
            functools.partial(reduce_kernel, (batch, head_dim)),
            name='project_and_sum',
            out_shape=[pltpu.VMEM(shape, BF16) for shape in out_shapes],
            in_specs=[any_spec, vmem_spec, vmem_spec, vmem_spec, any_spec, any_spec],
            out_specs=[vmem_spec] * 3,
            scratch_shapes=[
                pltpu.VMEM((quarter, model_dim), BF16),
                pltpu.VMEM((4, quarter, 2 * head_dim), BF16),
                pltpu.VMEM((2, quarter, 4, head_dim), F32),
                pltpu.VMEM((q_width, model_dim), BF16),
                pltpu.VMEM((ffn, model_dim), BF16),
                pltpu.VMEM((pieces, batch, PIECE), F32),
                pltpu.VMEM((pieces, 2 * quarter, PIECE), F32),
                pltpu.VMEM((pieces, 2 * quarter, PIECE), F32),
                pltpu.VMEM((pieces, quarter, PIECE), F32),
                dma((1,)),
                dma((2, pieces)),
                dma((3,)), dma((3,)),
            ] + [dma((pieces,))] * 10,
            compiler_params=pltpu.CompilerParams(collective_id=0, has_side_effects=True, vmem_limit_bytes=48 << 20),
        )(tokens, hidden, attended, kv_new, w_out, w_down)

    in_specs = (P('replica', None), P('replica'), P('replica', None, None, None), P('replica', None, None, None), P(None), P(None, 'model'), P(None, None), P(None, None), P('model', None), P(None, 'model'), P(None, 'model'), P('model', None))
    out_specs = (P('replica', None), P(('replica', 'model'), None, None), P(('replica', 'model'), None, None))
    return jax.shard_map(local_step, mesh=mesh, in_specs=in_specs, out_specs=out_specs, check_vma=False)
```

profile of v0, /device:TPU:0, one launch (start us, length us, event | category | flops | bytes accessed | tf_op | source)
XLA Modules:
  0.0 36.7 jit_solution(16230445129746902728)
XLA Ops:
  0.6 0.0 copy-start
  0.6 0.0 copy-start.1
  0.7 15.5 %attend_and_gate.1 = (bf16[128,2304]{1,0:T(8,128)(2,1)S(1)}, bf16[128,512]{1,0:T(8,128)(2,1)S(1)}, bf16[128,512]{1,0:T(8,128)(2,1)S(1)}) custom-call(s32[1,128]{1,0:T(1,128)} %bitcast.1, bf16[128,2304]{1,0:T(8,128)(2,1)} %x_hbm.3, bf16[2304]{0:T(1024)(128)(2,1)} %gain_hbm.1, bf16[128,4,512,256]{3,2,1,0:T(8,128)(2,1)} %k_hbm.1, ...), custom_call_target="tpu_custom_call" | custom-call | tf_op jit(solution)/shard_map/attend_and_gate/pallas_call | solution.py:371
  16.1 0.0 copy-done
  16.1 0.0 copy-done.1
  16.1 18.5 %project_and_sum.1 = (bf16[128,2304]{1,0:T(8,128)(2,1)S(1)}, bf16[32,4,256]{2,1,0:T(4,128)(2,1)S(1)}, bf16[32,4,256]{2,1,0:T(4,128)(2,1)S(1)}) custom-call(bf16[128,2304]{1,0:T(8,128)(2,1)S(1)} %copy-done, bf16[128,2304]{1,0:T(8,128)(2,1)S(1)} %get-tuple-element.6.u_v, bf16[128,512]{1,0:T(8,128)(2,1)S(1)} %get-tuple-element.7.o_v, ...), custom_call_target="tpu_custom_call" | custom-call | tf_op jit(solution)/shard_map/project_and_sum/pallas_call | solution.py:415
  34.6 0.8 %copy.18 = bf16[128,2304]{1,0:T(8,128)(2,1)} copy(bf16[128,2304]{1,0:T(8,128)(2,1)S(1)} %get-tuple-element.9) | data formatting | bytes 1179648
  35.5 0.6 %copy.19 = bf16[32,4,256]{2,1,0:T(4,128)(2,1)} copy(bf16[32,4,256]{2,1,0:T(4,128)(2,1)S(1)} %get-tuple-element.10) | data formatting | bytes 131072
  36.1 0.6 %copy.20 = bf16[32,4,256]{2,1,0:T(4,128)(2,1)} copy(bf16[32,4,256]{2,1,0:T(4,128)(2,1)S(1)} %get-tuple-element.11) | data formatting | bytes 131072
Async XLA Ops:
  0.6 15.5 %copy-start = (bf16[128,2304]{1,0:T(8,128)(2,1)S(1)}, bf16[128,2304]{1,0:T(8,128)(2,1)}, u32[]{:S(2)}) copy-start(bf16[128,2304]{1,0:T(8,128)(2,1)} %x_hbm.3) | copy-start | bytes 1769476
  0.6 15.5 %copy-start.1 = (bf16[512,2304]{1,0:T(8,128)(2,1)S(1)}, bf16[512,2304]{1,0:T(8,128)(2,1)}, u32[]{:S(2)}) copy-start(bf16[512,2304]{1,0:T(8,128)(2,1)} %wo_hbm.1) | copy-start | bytes 7077892
where the time goes:
time: 36.4 us; the launch traced here: 36.7 us
  Pallas kernels  34 us (93%)
  local copies, waits for them, and re-layouts  2.08 us (6%)
  between operations  0.68 us (2%)
    pallas_call x1, Pallas kernels, local_step(): pl.pallas_call(functools.partial(reduce_kernel, (batch, head_dim)), name=...  18.5 us
    pallas_call x1, Pallas kernels, local_step(): pl.pallas_call(functools.partial(local_kernel, (batch, model_dim, head_di...  15.5 us
    unnamed x7, local copies, waits for them, and re-layouts  2.08 us

commit v1 on v0

--- a/solution.py
+++ b/solution.py
@@ -16,10 +16,10 @@
 FIRST = 32
 GROUP = 8
 CHUNK = 128
-UNROLL = 8
-SLOTS = 12
+UNROLL = 16
+SLOTS = 6
 COLS = 256
-PIECE = 384
+WIDTHS = (256, 256, 512, 512, 512, 256)
 
 
 def iota(shape, dim):
@@ -44,7 +44,7 @@
 def local_kernel(dims, len_hbm, x_hbm, gain_hbm, k_hbm, v_hbm, wq_hbm, wk_hbm, wv_hbm, wg_hbm, wu_hbm,
                  u_ref, o_ref, kv_ref,
                  len_s, len_v, x_v, gain_v, wq_v, wk_v, wv_v, wg_v, wu_v, kfirst, vfirst, kbuf, vbuf, h_v,
-                 tile_s, q_rows, len_rows, s_first, s_buf, snew_v, vnew_v, m_v, l_v, acc_v,
+                 tile_s, size_s, q_rows, len_rows, s_first, s_buf, snew_v, vnew_v, m_v, l_v, acc_v,
                  sems, wsems, fsems, ksems, vsems):
     batch, model_dim, head_dim, context = dims
     half = head_dim // 2
@@ -52,14 +52,14 @@
     groups = batch // GROUP
     me = lax.axis_index('model')
     n_pieces = wg_v.shape[0]
-    last_start = context - CHUNK
+    blocks = CHUNK // FIRST
 
     def piece_copy(hbm, buf, n, which):
         return pltpu.make_async_copy(hbm.at[:, pl.ds(n * COLS, COLS)], buf.at[n], wsems.at[which, n])
 
     def first_copy(hbm, buf, which, n):
         seqs = pl.ds(n * (batch // 2), batch // 2)
-        return pltpu.make_async_copy(hbm.at[seqs, me, pl.ds(0, FIRST), :], buf.at[seqs], fsems.at[which, n])
+        return pltpu.make_async_copy(hbm.at[seqs, me, 0], buf.at[seqs], fsems.at[which, n])
 
     head_col = pl.multiple_of(me * head_dim, 128)
     small = [
@@ -81,6 +81,7 @@
         piece_copy(wg_hbm, wg_v, n, 0).start(priority=1)
         piece_copy(wu_hbm, wu_v, n, 1).start(priority=1)
 
+    vbuf[...] = jnp.zeros_like(vbuf)
     small[0].wait()
 
     def fill(r, t):
@@ -97,11 +98,16 @@
 
     def issue(hbm, buf, bsems, body):
         slot = lax.rem(body, SLOTS)
+        total = 0
         for j in range(UNROLL):
             code = tile_s[body * UNROLL + j]
-            start = jnp.minimum(FIRST + (code & 7) * CHUNK, last_start)
-            pltpu.make_async_copy(hbm.at[lax.shift_right_logical(code, 3), me, pl.ds(pl.multiple_of(start, FIRST), CHUNK), :],
-                                  buf.at[slot, j], bsems.at[slot]).start()
+            b = lax.shift_right_logical(code, 3)
+            start = jnp.minimum(1 + (code & 7) * blocks, context // FIRST - 1)
+            end = lax.shift_right_logical(len_s[0, b] + (FIRST - 1), FIRST.bit_length() - 1)
+            count = jnp.clip(end - start, 1, blocks)
+            pltpu.make_async_copy(hbm.at[b, me, pl.ds(start, count)], buf.at[slot, pl.ds(j * blocks, count)], bsems.at[slot]).start()
+            total += count
+        size_s[body] = total
 
     def issue_both(body, _):
         issue(k_hbm, kbuf, ksems, body)
@@ -110,7 +116,8 @@
 
     def wait_body(buf, bsems, body):
         slot = lax.rem(body, SLOTS)
-        pltpu.make_async_copy(buf.at[slot], buf.at[slot], bsems.at[slot]).wait()
+        filled = buf.at[slot, pl.ds(0, size_s[body])]
+        pltpu.make_async_copy(filled, filled, bsems.at[slot]).wait()
 
     lax.fori_loop(0, jnp.minimum(bodies, SLOTS), issue_both, 0)
 
@@ -177,9 +184,8 @@
         scores = []
         for j in range(UNROLL):
             i, row, begin = tile_of(body * UNROLL + j)
-            s = nt_dot(q_rows[pl.ds(row, rows), :], kbuf[slot, j])
-            position = lane + jnp.minimum(begin, last_start)
-            valid = (sub == i) & (position >= begin) & (position.astype(F32) < len_rows[pl.ds(row, rows), :])
+            s = nt_dot(q_rows[pl.ds(row, rows), :], kbuf[slot, j * blocks:(j + 1) * blocks].reshape(CHUNK, head_dim))
+            valid = (sub == i) & ((lane + begin).astype(F32) < len_rows[pl.ds(row, rows), :])
             scores.append((row, jnp.where(valid, s * scale, MASK_VALUE)))
         for j, (row, s) in enumerate(scores):
             s_buf[body * UNROLL + j] = s
@@ -209,7 +215,7 @@
         for j in range(UNROLL):
             _, row, _ = tile_of(body * UNROLL + j)
             p = jnp.exp(s_buf[body * UNROLL + j] - m_v[pl.ds(row, rows), :])
-            mixed.append((row, p, nn_dot(p.astype(BF16), vbuf[slot, j])))
+            mixed.append((row, p, nn_dot(p.astype(BF16), vbuf[slot, j * blocks:(j + 1) * blocks].reshape(CHUNK, head_dim))))
         for row, p, o in mixed:
             l_v[pl.ds(row, rows), :] += p
             acc_v[pl.ds(row, rows), :] += o
@@ -242,11 +248,16 @@
                   sems, wsems, kv_send, kv_recv, rs_send, rs_recv, xs_send, xs_recv, gx_send, gx_recv, gs_send, gs_recv, gf_send, gf_recv):
     batch, head_dim = dims
     quarter = batch // 4
-    pieces = part.shape[0]
+    pieces = len(WIDTHS)
+
+    def cols_of(n):
+        return pl.ds(sum(WIDTHS[:n]), WIDTHS[n])
+
     me = lax.axis_index('model')
     chip, core = me // 2, me % 2
     sibling = chip * 2 + (1 - core)
     across = (1 - chip) * 2 + core
+    diagonal = (1 - chip) * 2 + (1 - core)
 
     def rows_of(chip_, core_):
         return pl.multiple_of(core_ * (2 * quarter) + chip_ * quarter, quarter)
@@ -256,7 +267,7 @@
     sib_half = pl.multiple_of((1 - core) * (2 * quarter), 2 * quarter)
 
     def weight_copies(n):
-        cols = pl.ds(n * PIECE, PIECE)
+        cols = cols_of(n)
         return (pltpu.make_async_copy(wo_hbm.at[:, cols], wo_v.at[:, cols], wsems.at[0, n]),
                 pltpu.make_async_copy(wd_hbm.at[:, cols], wd_v.at[:, cols], wsems.at[1, n]))
 
@@ -286,13 +297,13 @@
                                             device_id={'model': to}, device_id_type=pl.DeviceIdType.MESH)
 
     def rs(n):
-        return remote(part.at[n, pl.ds(sib_half, 2 * quarter), :], from_sib.at[n], rs_send, rs_recv, n, sibling)
+        return remote(part.at[pl.ds(sib_half, 2 * quarter), cols_of(n)], from_sib.at[:, cols_of(n)], rs_send, rs_recv, n, sibling)
 
     def xs(n):
-        return remote(half_sum.at[n, pl.ds(pl.multiple_of((1 - chip) * quarter, quarter), quarter), :], from_chip.at[n], xs_send, xs_recv, n, across)
+        return remote(half_sum.at[pl.ds(pl.multiple_of((1 - chip) * quarter, quarter), quarter), cols_of(n)], from_chip.at[:, cols_of(n)], xs_send, xs_recv, n, across)
 
     def y_piece(row, n):
-        return y_v.at[pl.ds(row, quarter), pl.ds(n * PIECE, PIECE)]
+        return y_v.at[pl.ds(row, quarter), cols_of(n)]
 
     def gx(n):
         return remote(y_piece(own, n), y_piece(own, n), gx_send, gx_recv, n, across)
@@ -301,31 +312,36 @@
         return remote(y_piece(own, n), y_piece(own, n), gs_send, gs_recv, n, sibling)
 
     def gf(n):
+        if n == pieces - 1:
+            return remote(y_piece(own, n), y_piece(own, n), gf_send, gf_recv, n, diagonal)
         other = rows_of(1 - chip, core)
         return remote(y_piece(other, n), y_piece(other, n), gf_send, gf_recv, n, sibling)
 
     def sum_chip(n):
         rs(n).wait_recv()
-        half_sum[n] = part[n, pl.ds(own_half, 2 * quarter), :] + from_sib[n]
+        half_sum[:, cols_of(n)] = part[pl.ds(own_half, 2 * quarter), cols_of(n)] + from_sib[:, cols_of(n)]
         xs(n).start()
 
     def finish(n):
         xs(n).wait_recv()
-        cols = slice(n * PIECE, (n + 1) * PIECE)
-        mine = half_sum[n, pl.ds(pl.multiple_of(chip * quarter, quarter), quarter), :] + from_chip[n]
+        cols = cols_of(n)
+        mine = half_sum[pl.ds(pl.multiple_of(chip * quarter, quarter), quarter), cols] + from_chip[:, cols]
         y_v[pl.ds(own, quarter), cols] = (x_v[:, cols].astype(F32) + mine).astype(BF16)
         gx(n).start()
+        if n == pieces - 1:
+            gf(n).start()
         gs(n).start()
 
     def forward(n):
         gx(n).wait_recv()
-        gf(n).start()
+        if n < pieces - 1:
+            gf(n).start()
 
     for n in range(pieces):
         for copy in weight_copies(n):
             copy.wait()
-        cols = slice(n * PIECE, (n + 1) * PIECE)
-        part[n] = nn_dot(o_v[...], wo_v[:, cols]) + nn_dot(u_v[...], wd_v[:, cols])
+        cols = cols_of(n)
+        part[:, cols] = nn_dot(o_v[...], wo_v[:, cols]) + nn_dot(u_v[...], wd_v[:, cols])
         rs(n).start()
         if n >= 1:
             sum_chip(n - 1)
@@ -353,6 +369,14 @@
     for n in range(pieces):
         for copy in (rs(n), xs(n), gx(n), gs(n), gf(n)):
             copy.wait_send()
+
+
+def write_kernel(y_v, kn_v, vn_v, y_hbm, kn_hbm, vn_hbm, sems):
+    copies = [pltpu.make_async_copy(src, dst, sems.at[i]) for i, (src, dst) in enumerate([(y_v, y_hbm), (kn_v, kn_hbm), (vn_v, vn_hbm)])]
+    for copy in copies:
+        copy.start()
+    for copy in copies:
+        copy.wait()
 
 
 def solution(mesh):
@@ -368,6 +392,7 @@
         dma = pltpu.SemaphoreType.DMA
 
         pieces = ffn // COLS
+        in_blocks = (batch, kv_heads, context // FIRST, FIRST, head_dim)
         hidden, attended, kv_new = pl.pallas_call(
             functools.partial(local_kernel, (batch, model_dim, head_dim, context)),
             name='attend_and_gate',
@@ -386,10 +411,11 @@
                 pltpu.VMEM((pieces, model_dim, COLS), BF16),
                 pltpu.VMEM((batch, FIRST, head_dim), BF16),
                 pltpu.VMEM((batch, FIRST, head_dim), BF16),
-                pltpu.VMEM((SLOTS, UNROLL, CHUNK, head_dim), BF16),
-                pltpu.VMEM((SLOTS, UNROLL, CHUNK, head_dim), BF16),
+                pltpu.VMEM((SLOTS, UNROLL * CHUNK // FIRST, FIRST, head_dim), BF16),
+                pltpu.VMEM((SLOTS, UNROLL * CHUNK // FIRST, FIRST, head_dim), BF16),
                 pltpu.VMEM((batch, model_dim), BF16),
                 pltpu.SMEM((max_tiles,), jnp.int32),
+                pltpu.SMEM((max_tiles // UNROLL + 1,), jnp.int32),
                 pltpu.VMEM((rows, head_dim), BF16),
                 pltpu.VMEM((rows, 128), F32),
                 pltpu.VMEM((batch // GROUP, 2 * GROUP, GROUP * FIRST), F32),
@@ -406,13 +432,13 @@
                 dma((SLOTS,)),
             ],
             compiler_params=pltpu.CompilerParams(has_side_effects=True, vmem_limit_bytes=54 << 20),
-        )(lengths.reshape(1, batch), tokens, norm_gain, k_cache, v_cache, w_query, w_key, w_value, w_gate, w_up)
+        )(lengths.reshape(1, batch), tokens, norm_gain, k_cache.reshape(in_blocks), v_cache.reshape(in_blocks), w_query, w_key, w_value, w_gate, w_up)
 
         quarter = batch // 4
-        pieces = model_dim // PIECE
+        pieces = len(WIDTHS)
         new_shape = (quarter, kv_heads, head_dim)
         out_shapes = [(batch, model_dim), new_shape, new_shape]
-        return pl.pallas_call(
+        outs = pl.pallas_call(
             functools.partial(reduce_kernel, (batch, head_dim)),
             name='project_and_sum',
             out_shape=[pltpu.VMEM(shape, BF16) for shape in out_shapes],
@@ -424,16 +450,25 @@
                 pltpu.VMEM((2, quarter, 4, head_dim), F32),
                 pltpu.VMEM((q_width, model_dim), BF16),
                 pltpu.VMEM((ffn, model_dim), BF16),
-                pltpu.VMEM((pieces, batch, PIECE), F32),
-                pltpu.VMEM((pieces, 2 * quarter, PIECE), F32),
-                pltpu.VMEM((pieces, 2 * quarter, PIECE), F32),
-                pltpu.VMEM((pieces, quarter, PIECE), F32),
+                pltpu.VMEM((batch, model_dim), F32),
+                pltpu.VMEM((2 * quarter, model_dim), F32),
+                pltpu.VMEM((2 * quarter, model_dim), F32),
+                pltpu.VMEM((quarter, model_dim), F32),
                 dma((1,)),
                 dma((2, pieces)),
                 dma((3,)), dma((3,)),
             ] + [dma((pieces,))] * 10,
             compiler_params=pltpu.CompilerParams(collective_id=0, has_side_effects=True, vmem_limit_bytes=48 << 20),
         )(tokens, hidden, attended, kv_new, w_out, w_down)
+        return pl.pallas_call(
+            write_kernel,
+            name='write_results',
+            out_shape=[jax.ShapeDtypeStruct(shape, BF16) for shape in out_shapes],
+            in_specs=[vmem_spec] * 3,
+            out_specs=[any_spec] * 3,
+            scratch_shapes=[dma((3,))],
+            compiler_params=pltpu.CompilerParams(has_side_effects=True, vmem_limit_bytes=4 << 20),
+        )(*outs)
 
     in_specs = (P('replica', None), P('replica'), P('replica', None, None, None), P('replica', None, None, None), P(None), P(None, 'model'), P(None, None), P(None, None), P('model', None), P(None, 'model'), P(None, 'model'), P('model', None))
     out_specs = (P('replica', None), P(('replica', 'model'), None, None), P(('replica', 'model'), None, None))

time: 36.4 us -> 33.2 us (0.912); the launches traced: 36.7 us -> 33.1 us
  local copies, waits for them, and re-layouts: 2.08 us -> 0.01 us
  Pallas kernels: 34 us -> 32.4 us
    unnamed x7 -> x4, local copies, waits for them, and re-layouts: 2.08 us -> 0.01 us
    pallas_call x1, Pallas kernels: 15.5 us -> 13.4 us  [local_step(): pl.pallas_call(functools.partial(local_kernel, (batch, model_dim, head_di...]
    pallas_call x0 -> x1, Pallas kernels: none -> 0.87 us  [local_step(): pl.pallas_call(write_kernel, name='write_results', out_shape=[jax.ShapeDt...]
    pallas_call x1, Pallas kernels: 18.5 us -> 18.1 us  [local_step(): pl.pallas_call(functools.partial(reduce_kernel, (batch, head_dim)), name=...]
where the time goes in v1:
time: 33.2 us; the launch traced here: 33.1 us
  Pallas kernels  32.4 us (98%)
  between operations  0.68 us (2%)
    pallas_call x1, Pallas kernels, local_step(): pl.pallas_call(functools.partial(reduce_kernel, (batch, head_dim)), name=...  18.1 us
    pallas_call x1, Pallas kernels, local_step(): pl.pallas_call(functools.partial(local_kernel, (batch, model_dim, head_di...  13.4 us
    pallas_call x1, Pallas kernels, local_step(): pl.pallas_call(write_kernel, name='write_results', out_shape=[jax.ShapeDt...  0.87 us

profile of v1, /device:TPU:0, one launch (start us, length us, event | category | flops | bytes accessed | tf_op | source)
XLA Modules:
  0.0 33.1 jit_solution(12957477047876507662)
XLA Ops:
  0.6 0.0 copy-start
  0.6 0.0 copy-start.1
  0.7 13.4 %attend_and_gate.1 = (bf16[128,2304]{1,0:T(8,128)(2,1)S(1)}, bf16[128,512]{1,0:T(8,128)(2,1)S(1)}, bf16[128,512]{1,0:T(8,128)(2,1)S(1)}) custom-call(s32[1,128]{1,0:T(1,128)} %bitcast.3, bf16[128,2304]{1,0:T(8,128)(2,1)} %x_hbm.3, bf16[2304]{0:T(1024)(128)(2,1)} %gain_hbm.1, bf16[128,4,16,32,256]{4,3,2,1,0:T(8,128)(2,1)} %bitcast.1.k_hbm, ...), custom_call_target="tpu_custom_call" | custom-call | tf_op jit(solution)/shard_map/attend_and_gate/pallas_call | solution.py:396
  14.1 0.0 copy-done
  14.1 0.0 copy-done.1
  14.1 18.1 %project_and_sum.1 = (bf16[128,2304]{1,0:T(8,128)(2,1)S(1)}, bf16[32,4,256]{2,1,0:T(4,128)(2,1)S(1)}, bf16[32,4,256]{2,1,0:T(4,128)(2,1)S(1)}) custom-call(bf16[128,2304]{1,0:T(8,128)(2,1)S(1)} %copy-done, bf16[128,2304]{1,0:T(8,128)(2,1)S(1)} %get-tuple-element.9.u_v, bf16[128,512]{1,0:T(8,128)(2,1)S(1)} %get-tuple-element.10.o_v, ...), custom_call_target="tpu_custom_call" | custom-call | tf_op jit(solution)/shard_map/project_and_sum/pallas_call | solution.py:441
  32.2 0.9 %write_results.1 = (bf16[128,2304]{1,0:T(8,128)(2,1)}, bf16[32,4,256]{2,1,0:T(4,128)(2,1)}, bf16[32,4,256]{2,1,0:T(4,128)(2,1)}) custom-call(bf16[128,2304]{1,0:T(8,128)(2,1)S(1)} %get-tuple-element.12.y_v, bf16[32,4,256]{2,1,0:T(4,128)(2,1)S(1)} %get-tuple-element.13.kn_v, bf16[32,4,256]{2,1,0:T(4,128)(2,1)S(1)} %get-tuple-element.14.vn_v), custom_call_target="tpu_custom_call" | custom-call | tf_op jit(solution)/shard_map/write_results/pallas_call | solution.py:463
Async XLA Ops:
  0.6 13.5 %copy-start = (bf16[128,2304]{1,0:T(8,128)(2,1)S(1)}, bf16[128,2304]{1,0:T(8,128)(2,1)}, u32[]{:S(2)}) copy-start(bf16[128,2304]{1,0:T(8,128)(2,1)} %x_hbm.3) | copy-start | bytes 1769476
  0.6 13.5 %copy-start.1 = (bf16[512,2304]{1,0:T(8,128)(2,1)S(1)}, bf16[512,2304]{1,0:T(8,128)(2,1)}, u32[]{:S(2)}) copy-start(bf16[512,2304]{1,0:T(8,128)(2,1)} %wo_hbm.1) | copy-start | bytes 7077892

commit v2 on v1

--- a/solution.py
+++ b/solution.py
@@ -18,7 +18,7 @@
 CHUNK = 128
 UNROLL = 16
 SLOTS = 6
-COLS = 256
+GATE_WIDTHS = (768, 768, 512, 256)
 WIDTHS = (256, 256, 512, 512, 512, 256)
 
 
@@ -51,11 +51,14 @@
     rows = 2 * GROUP
     groups = batch // GROUP
     me = lax.axis_index('model')
-    n_pieces = wg_v.shape[0]
+    n_pieces = len(GATE_WIDTHS)
     blocks = CHUNK // FIRST
 
+    def gate_cols(n):
+        return pl.ds(sum(GATE_WIDTHS[:n]), GATE_WIDTHS[n])
+
     def piece_copy(hbm, buf, n, which):
-        return pltpu.make_async_copy(hbm.at[:, pl.ds(n * COLS, COLS)], buf.at[n], wsems.at[which, n])
+        return pltpu.make_async_copy(hbm.at[:, gate_cols(n)], buf.at[:, gate_cols(n)], wsems.at[which, n])
 
     def first_copy(hbm, buf, which, n):
         seqs = pl.ds(n * (batch // 2), batch // 2)
@@ -141,18 +144,18 @@
     h_v[...] = (x * lax.rsqrt(mean_sq + NORM_EPS) * gain_v[...].astype(F32).reshape(1, model_dim)).astype(BF16)
 
     small[4].wait()
+    h = h_v[...]
+    q = nn_dot(h, wq_v[...])
+    q_heads = [rope(q[:, n * head_dim:(n + 1) * head_dim]).astype(F32) for n in range(2)]
+    q_rows[...] = interleave(*q_heads).astype(BF16)
     small[5].wait()
     small[6].wait()
-    h = h_v[...]
-    q = nn_dot(h, wq_v[...])
     k_new = rope(nn_dot(h, wk_v[...]))
     v_new = nn_dot(h, wv_v[...]).astype(BF16)
     kv_ref[:, :head_dim] = k_new
     kv_ref[:, head_dim:] = v_new
     vnew_v[...] = v_new.astype(F32)
     scale = head_dim ** -0.5
-    q_heads = [rope(q[:, n * head_dim:(n + 1) * head_dim]).astype(F32) for n in range(2)]
-    q_rows[...] = interleave(*q_heads).astype(BF16)
     k_wide = k_new.astype(F32)
     s_new = [jnp.broadcast_to(jnp.sum(qh * k_wide, axis=1, keepdims=True) * scale, (batch, 128)) for qh in q_heads]
     snew_v[...] = interleave(*s_new)
@@ -237,9 +240,9 @@
     for n in range(n_pieces):
         piece_copy(wg_hbm, wg_v, n, 0).wait()
         piece_copy(wu_hbm, wu_v, n, 1).wait()
-        gate = nn_dot(h_v[...], wg_v[n])
-        up = nn_dot(h_v[...], wu_v[n])
-        u_ref[:, n * COLS:(n + 1) * COLS] = (gate * jax.nn.sigmoid(gate) * up).astype(BF16)
+        gate = nn_dot(h_v[...], wg_v[:, gate_cols(n)])
+        up = nn_dot(h_v[...], wu_v[:, gate_cols(n)])
+        u_ref[:, gate_cols(n)] = (gate * jax.nn.sigmoid(gate) * up).astype(BF16)
 
 
 def reduce_kernel(dims, x_hbm, u_v, o_v, kv_v, wo_hbm, wd_hbm,
@@ -391,7 +394,7 @@
         vmem_spec = pl.BlockSpec(memory_space=pltpu.VMEM)
         dma = pltpu.SemaphoreType.DMA
 
-        pieces = ffn // COLS
+        pieces = len(GATE_WIDTHS)
         in_blocks = (batch, kv_heads, context // FIRST, FIRST, head_dim)
         hidden, attended, kv_new = pl.pallas_call(
             functools.partial(local_kernel, (batch, model_dim, head_dim, context)),
@@ -407,8 +410,8 @@
                 pltpu.VMEM((model_dim, q_width), BF16),
                 pltpu.VMEM((model_dim, head_dim), BF16),
                 pltpu.VMEM((model_dim, head_dim), BF16),
-                pltpu.VMEM((pieces, model_dim, COLS), BF16),
-                pltpu.VMEM((pieces, model_dim, COLS), BF16),
+                pltpu.VMEM((model_dim, ffn), BF16),
+                pltpu.VMEM((model_dim, ffn), BF16),
                 pltpu.VMEM((batch, FIRST, head_dim), BF16),
                 pltpu.VMEM((batch, FIRST, head_dim), BF16),
                 pltpu.VMEM((SLOTS, UNROLL * CHUNK // FIRST, FIRST, head_dim), BF16),

time: 33.2 us -> 32.5 us (0.979)
  Pallas kernels: 32.4 us -> 31.7 us
    pallas_call x1, Pallas kernels: 13.4 us -> 12.7 us  [local_step(): pl.pallas_call(functools.partial(local_kernel, (batch, model_dim, head_di...]
where the time goes in v2:
time: 32.5 us; the launch traced here: 32.4 us
  Pallas kernels  31.7 us (98%)
  between operations  0.68 us (2%)
    pallas_call x1, Pallas kernels, local_step(): pl.pallas_call(functools.partial(reduce_kernel, (batch, head_dim)), name=...  18.1 us
    pallas_call x1, Pallas kernels, local_step(): pl.pallas_call(functools.partial(local_kernel, (batch, model_dim, head_di...  12.7 us
    pallas_call x1, Pallas kernels, local_step(): pl.pallas_call(write_kernel, name='write_results', out_shape=[jax.ShapeDt...  0.87 us

profile of v2, /device:TPU:0, one launch (start us, length us, event | category | flops | bytes accessed | tf_op | source)
XLA Modules:
  0.0 32.4 jit_solution(12210840336567014268)
XLA Ops:
  0.6 0.0 copy-start
  0.6 0.0 copy-start.1
  0.7 12.7 %attend_and_gate.1 = (bf16[128,2304]{1,0:T(8,128)(2,1)S(1)}, bf16[128,512]{1,0:T(8,128)(2,1)S(1)}, bf16[128,512]{1,0:T(8,128)(2,1)S(1)}) custom-call(s32[1,128]{1,0:T(1,128)} %bitcast.3, bf16[128,2304]{1,0:T(8,128)(2,1)} %x_hbm.3, bf16[2304]{0:T(1024)(128)(2,1)} %gain_hbm.1, bf16[128,4,16,32,256]{4,3,2,1,0:T(8,128)(2,1)} %bitcast.1.k_hbm, ...), custom_call_target="tpu_custom_call" | custom-call | tf_op jit(solution)/shard_map/attend_and_gate/pallas_call | solution.py:399
  13.4 0.0 copy-done
  13.4 0.0 copy-done.1
  13.4 18.1 %project_and_sum.1 = (bf16[128,2304]{1,0:T(8,128)(2,1)S(1)}, bf16[32,4,256]{2,1,0:T(4,128)(2,1)S(1)}, bf16[32,4,256]{2,1,0:T(4,128)(2,1)S(1)}) custom-call(bf16[128,2304]{1,0:T(8,128)(2,1)S(1)} %copy-done, bf16[128,2304]{1,0:T(8,128)(2,1)S(1)} %get-tuple-element.9.u_v, bf16[128,512]{1,0:T(8,128)(2,1)S(1)} %get-tuple-element.10.o_v, ...), custom_call_target="tpu_custom_call" | custom-call | tf_op jit(solution)/shard_map/project_and_sum/pallas_call | solution.py:444
  31.5 0.9 %write_results.1 = (bf16[128,2304]{1,0:T(8,128)(2,1)}, bf16[32,4,256]{2,1,0:T(4,128)(2,1)}, bf16[32,4,256]{2,1,0:T(4,128)(2,1)}) custom-call(bf16[128,2304]{1,0:T(8,128)(2,1)S(1)} %get-tuple-element.12.y_v, bf16[32,4,256]{2,1,0:T(4,128)(2,1)S(1)} %get-tuple-element.13.kn_v, bf16[32,4,256]{2,1,0:T(4,128)(2,1)S(1)} %get-tuple-element.14.vn_v), custom_call_target="tpu_custom_call" | custom-call | tf_op jit(solution)/shard_map/write_results/pallas_call | solution.py:466
Async XLA Ops:
  0.6 12.8 %copy-start = (bf16[128,2304]{1,0:T(8,128)(2,1)S(1)}, bf16[128,2304]{1,0:T(8,128)(2,1)}, u32[]{:S(2)}) copy-start(bf16[128,2304]{1,0:T(8,128)(2,1)} %x_hbm.3) | copy-start | bytes 1769476
  0.6 12.8 %copy-start.1 = (bf16[512,2304]{1,0:T(8,128)(2,1)S(1)}, bf16[512,2304]{1,0:T(8,128)(2,1)}, u32[]{:S(2)}) copy-start(bf16[512,2304]{1,0:T(8,128)(2,1)} %wo_hbm.1) | copy-start | bytes 7077892
